TPU v7x, 32 devices: a whole 2x2x4 slice. The times are simulated.
32 devices in a mesh: grp: 2 (over y), tgt: 4 (over z), src: 4 (over x, core).
Axes of the slice: x: 2, y: 2, z: 4, core: 2. Of those that a mesh axis runs over, the one named last changes fastest.
Arguments:
- target_rows: bfloat16 [2048, 4608], P(('grp', 'tgt', 'src')), parts along dimension 0, may hold values from -6 to 6
- target_pos: int32 [2048], P(('grp', 'tgt')), parts along dimension 0, may hold values from 0 to 255
- decoder_rows: bfloat16 [512, 4608], P(('grp', 'tgt', 'src')), parts along dimension 0, may hold values from -0.09375 to 0.09375
- source_pos: int32 [512], P('grp'), parts along dimension 0, may hold values from 0 to 255
- out_proj: bfloat16 [32, 4608, 128], P('src', 'tgt'), may hold values from -0.09375 to 0.09375
- value_proj: bfloat16 [16, 4608, 128], P('src'), may hold values from -1 to 1
- attention: bfloat16 [64, 256, 256], P(('grp', 'src'), 'tgt'), parts along dimension 0, may hold values from 0 to 1, as said below
- tile_pattern: int32 [8, 4], P('grp'), parts along dimension 0, may hold values from 0 to 1, as said below
Outputs:
- edges: bfloat16 [512, 1024], P(('grp', 'src'), 'tgt'), parts along dimension 0
There are 2 independent parts, one for each index of `grp`. A program takes and returns all parts, laid end to end along the dimension named above; an argument that names none is the same for every part. Nothing has to cross between parts.
Inputs may be any that keep to these rules, and one draw needn't show every extreme that they name: Each row attention[h, p, :] is a probability distribution over the keys 0 to p: zero beyond p, summing to one. tile_pattern[b, c] is 1 where the tile of edges between source block b and target block c is kept, else 0.
All inputs are finite; a program needn't handle non-finite values.
Results may differ from a plain program's by a relative error of at most 0.0057.
Values may be sent and summed in bfloat16 or wider, within the bound.
A program may use at most 64 MiB of HBM per device.

v0:
```python
import jax
import jax.numpy as jnp
from jax import lax
from jax.sharding import PartitionSpec as P


def passed_along(value, axis, steps):
    count = lax.axis_size(axis)
    pairs = [(source, (source + steps) % count) for source in range(count)]
    return lax.ppermute(value, axis, pairs)


def shards(
    target_rows, target_pos, decoder_rows, source_pos, out_proj, value_proj, attention, tile_pattern
):
    blocks = lax.axis_size("tgt")
    column = lax.axis_index("tgt")
    src_lane = lax.axis_index("src")
    full_targets, full_sources = (
        lax.all_gather(target_rows, "src", axis=0, tiled=True),
        lax.all_gather(decoder_rows, "src", axis=0, tiled=True),
    )
    tgt_dev = full_targets.shape[0]
    src_dev = full_sources.shape[0]
    sub_rows = decoder_rows.shape[0]
    heads_here = out_proj.shape[0]
    head_dim = out_proj.shape[2]
    groups_here = value_proj.shape[0]
    repeat = heads_here // groups_here
    read_sum = jnp.einsum(
        "td,hde->the",
        full_targets,
        lax.all_gather(out_proj, "tgt", axis=1, tiled=True),
        preferred_element_type=jnp.float32,
    )
    head_reads = read_sum.astype(jnp.bfloat16).reshape(tgt_dev, groups_here, repeat, head_dim)
    values = jnp.einsum("sd,gde->sge", full_sources, value_proj, preferred_element_type=jnp.float32)
    values = values.astype(jnp.bfloat16).reshape(src_dev, groups_here * head_dim)
    attn_table = lax.all_gather(attention, "tgt", axis=1, tiled=True)
    target_attn = jnp.take(attn_table, target_pos, axis=1)
    keyed_attn = jnp.transpose(target_attn, (0, 2, 1))

    def edge_tile(payload, block_index):
        decoder_part, value_part = payload
        key_positions = lax.dynamic_slice_in_dim(source_pos, block_index * src_dev, src_dev)
        weights = jnp.take(keyed_attn, key_positions, axis=1).astype(jnp.float32)
        scores = jnp.einsum(
            "sgd,tgrd->grst",
            value_part.reshape(src_dev, groups_here, head_dim),
            head_reads,
            preferred_element_type=jnp.float32,
        )
        scores = scores.reshape(heads_here, src_dev, tgt_dev)
        mixed_term = jnp.sum(weights * scores, axis=0)
        own_positions = lax.dynamic_slice_in_dim(key_positions, src_lane * sub_rows, sub_rows)
        same_place = (own_positions[:, None] == target_pos[None, :]).astype(jnp.float32)
        direct = (
            jnp.einsum("sd,td->st", decoder_part, full_targets, preferred_element_type=jnp.float32)
            * same_place
        )
        own_rows = lax.dynamic_slice_in_dim(mixed_term, src_lane * sub_rows, sub_rows, 0)
        return lax.dynamic_update_slice_in_dim(
            mixed_term, own_rows + direct, src_lane * sub_rows, 0
        )

    def place_tile(partial_value, payload, block_index):
        kept_flag = tile_pattern[block_index, column]
        piece_tile = edge_tile(payload, block_index) * kept_flag.astype(jnp.float32)
        return lax.dynamic_update_slice_in_dim(partial_value, piece_tile, block_index * src_dev, 0)

    own_block = (decoder_rows, values)
    partial_value = jnp.zeros((blocks * src_dev, tgt_dev), jnp.float32)
    partial_value = place_tile(partial_value, own_block, column)

    def cycle_turn(turn_index, state_carry):
        forward_block, backward_block, running = state_carry
        forward_block = passed_along((forward_block[0], forward_block[1]), "tgt", 1)
        backward_block = passed_along((backward_block[0], backward_block[1]), "tgt", -1)
        running = place_tile(running, forward_block, (column - turn_index) % blocks)
        running = place_tile(running, backward_block, (column + turn_index) % blocks)
        return (forward_block, backward_block, running)

    forward_block, backward_block, partial_value = lax.fori_loop(
        1, blocks // 2, cycle_turn, (own_block, own_block, partial_value)
    )
    forward_block = passed_along((forward_block[0], forward_block[1]), "tgt", 1)
    partial_value = place_tile(partial_value, forward_block, (column - blocks // 2) % blocks)
    summed = lax.psum_scatter(partial_value, "src", scatter_dimension=0, tiled=True)
    return summed.astype(jnp.bfloat16)


def solution(mesh):
    return jax.shard_map(
        shards,
        mesh=mesh,
        in_specs=(
            P(("grp", "tgt", "src"), None),
            P(("grp", "tgt")),
            P(("grp", "tgt", "src"), None),
            P("grp"),
            P("src", "tgt", None),
            P("src", None, None),
            P(("grp", "src"), "tgt", None),
            P("grp", None),
        ),
        out_specs=P(("grp", "src"), "tgt"),
        check_vma=False,
    )
```

profile of v0, /device:TPU:0, one launch (start us, length us, event | category | flops | bytes accessed | tf_op | source)
XLA Modules:
  0.0 277.3 jit_solution(18094460157816442848)
XLA Ops:
  6.5 1.9 copy.26
  8.5 0.7 all-gather.6.cloned.1.call-update
  9.2 0.7 all-gather.8.cloned.1.call-update
  10.0 5.1 %collective-permute-start.3 = (bf16[16,4608]{1,0:T(8,128)(2,1)S(1)}, bf16[16,4608]{1,0:T(8,128)(2,1)S(1)}, u32[]{:S(2)}, u32[]{:S(2)}) collective-permute-start(bf16[16,4608]{1,0:T(8,128)(2,1)S(1)} %copy-done.2), channel_id=1, source_target_pairs={{0,12},{4,0},{8,4},{12,8},{1,13},{5,1},{9,5},{13,9},{2,14},{6,2},{... | collective-permute-start | bytes 442376 | tf_op jit(solution)/shard_map/while/body/eval_jaxpr/ppermute | solution.py:10
  15.1 7.5 %all_gather.15 = bf16[64,4608]{1,0:T(8,128)(2,1)S(1)} all-gather(bf16[16,4608]{1,0:T(8,128)(2,1)S(1)} %copy-done.2), channel_id=1, replica_groups=mesh['grp'=2,'tgt'=4,'src'=4] {'src'}, dimensions={0}, use_global_device_ids=true | all-gather | bytes 737280 | tf_op jit(solution)/shard_map/all_gather | solution.py:21
  22.6 3.3 %convolution_convert_fusion = bf16[64,4,128]{2,0,1:T(8,128)(2,1)S(1)} fusion(bf16[4,4608,128]{2,1,0:T(8,128)(2,1)} %param.15, bf16[64,4608]{1,0:T(8,128)(2,1)S(1)} %all_gather.15), kind=kOutput, calls=%fused_computation.8 | convolution fusion | flops 302022656 | bytes 5373952 | tf_op jit(solution)/shard_map/sd,gde->sge/dot_general | solution.py:37
  26.0 3.9 %collective-permute-start.2 = (bf16[64,512]{1,0:T(8,128)(2,1)S(1)}, bf16[64,512]{1,0:T(8,128)(2,1)S(1)}, u32[]{:S(2)}, u32[]{:S(2)}) collective-permute-start(bf16[64,512]{1,0:T(8,128)(2,1)S(1)} %copy_bitcast_fusion), channel_id=1, source_target_pairs={{0,12},{4,0},{8,4},{12,8},{1,13},{5,1},{9,5},{13,9},{2,14},{6,2},{... | collective-permute-start | bytes 196616 | tf_op jit(solution)/shard_map/while/body/eval_jaxpr/ppermute | solution.py:10
  30.1 0.7 fusion.26
  33.4 4.4 %collective-permute-done = bf16[64,512]{1,0:T(8,128)(2,1)S(1)} collective-permute-done((bf16[64,512]{1,0:T(8,128)(2,1)S(1)}, bf16[64,512]{1,0:T(8,128)(2,1)S(1)}, u32[]{:S(2)}, u32[]{:S(2)}) %collective-permute-start) | collective-permute-done | bytes 65568 | tf_op jit(solution)/shard_map/while/body/eval_jaxpr/ppermute | solution.py:10
  37.8 1.1 collective-permute-start.4
  39.0 5.8 %collective-permute-done.4 = bf16[64,512]{1,0:T(8,128)(2,1)S(1)} collective-permute-done((bf16[64,512]{1,0:T(8,128)(2,1)S(1)}, bf16[64,512]{1,0:T(8,128)(2,1)S(1)}, u32[]{:S(2)}, u32[]{:S(2)}) %collective-permute-start.4) | collective-permute-done | bytes 65568 | tf_op jit(solution)/shard_map/ppermute | solution.py:10
  44.9 2.0 gather_fusion
  46.9 0.9 select_bitcast_fusion
  47.8 1.3 copy.27
  51.5 17.4 %all-gather.6.cloned.1.call-done = bf16[256,4608]{1,0:T(8,128)(2,1)} async-done(((bf16[64,4608]{1,0:T(8,128)(2,1)}), bf16[256,4608]{1,0:T(8,128)(2,1)}) %all-gather.6.cloned.1.call-update) | async-done | bytes 2359312 | tf_op jit(solution)/shard_map/all_gather | solution.py:20
  68.9 168.4 %all-gather.8.cloned.1.call-done = bf16[8,4608,128]{2,1,0:T(8,128)(2,1)} async-done(((bf16[8,1152,128]{2,1,0:T(8,128)(2,1)}), bf16[8,4608,128]{2,1,0:T(8,128)(2,1)}) %all-gather.8.cloned.1.call-update) | async-done | bytes 9437200 | tf_op jit(solution)/shard_map/all_gather | solution.py:33
  237.2 7.0 %fusion.2 = bf16[256,8,128]{2,0,1:T(8,128)(2,1)S(1)} fusion(bf16[8,4608,128]{2,1,0:T(8,128)(2,1)} %all-gather.8.cloned.1.call-done, bf16[256,4608]{1,0:T(8,128)(2,1)} %all-gather.6.cloned.1.call-done), kind=kOutput, calls=%fused_computation.7 | convolution fusion | flops 2416181248 | bytes 12320768 | tf_op jit(solution)/shard_map/td,hde->the/dot_general | solution.py:30
  246.3 0.7 fusion.12
  247.1 0.7 fusion.10
  248.3 0.7 fusion.8
  249.5 0.7 fusion.6
  250.3 0.7 copy-done.1
  251.0 18.4 %reduce-scatter.2.cloned.1.call-done = f32[64,256]{1,0:T(8,128)} async-done(((f32[256,256]{1,0:T(8,128)}), f32[64,256]{1,0:T(8,128)}) %reduce-scatter.2.cloned.1.call-update) | async-done | bytes 65552 | tf_op jit(solution)/shard_map/reduce_scatter | solution.py:88
  269.3 1.5 convert_element_type.69
  (54 shorter events, 6.1 us)
Async XLA Ops:
  6.5 3.4 %copy-start.2 = (bf16[16,4608]{1,0:T(8,128)(2,1)S(1)}, bf16[16,4608]{1,0:T(8,128)(2,1)}, u32[]{:S(2)}) copy-start(bf16[16,4608]{1,0:T(8,128)(2,1)} %param.12) | copy-start | bytes 442372
  6.5 38.4 %all-gather.4.cloned.1.call-start = ((), (), s32[]{:S(2)}) async-start(), calls=%async_computation.1 | async-start | bytes 1310720 | tf_op jit(solution)/shard_map/all_gather | solution.py:39
  8.4 60.4 %all-gather.6.cloned.1.call-start = ((), (), s32[]{:S(2)}) async-start(), calls=%async_computation.2 | async-start | bytes 2949120 | tf_op jit(solution)/shard_map/all_gather | solution.py:20
  9.2 228.1 %all-gather.8.cloned.1.call-start = ((), (), s32[]{:S(2)}) async-start(), calls=%async_computation.3 | async-start | bytes 11796480 | tf_op jit(solution)/shard_map/all_gather | solution.py:33
  9.9 259.4 %reduce-scatter.2.cloned.1.call-start = ((), (), s32[]{:S(2)}) async-start(), calls=%async_computation.4 | async-start | bytes 327680 | tf_op jit(solution)/shard_map/reduce_scatter | solution.py:88
  10.0 238.3 %collective-permute-start.3 = (bf16[16,4608]{1,0:T(8,128)(2,1)S(1)}, bf16[16,4608]{1,0:T(8,128)(2,1)S(1)}, u32[]{:S(2)}, u32[]{:S(2)}) collective-permute-start(bf16[16,4608]{1,0:T(8,128)(2,1)S(1)} %copy-done.2), channel_id=1, source_target_pairs={{0,12},{4,0},{8,4},{12,8},{1,13},{5,1},{9,5},{13,9},{2,14},{6,2},{... | collective-permute-start | bytes 442376 | tf_op jit(solution)/shard_map/while/body/eval_jaxpr/ppermute | solution.py:10
  15.1 29.7 %collective-permute-start.1 = (bf16[16,4608]{1,0:T(8,128)(2,1)S(1)}, bf16[16,4608]{1,0:T(8,128)(2,1)S(1)}, u32[]{:S(2)}, u32[]{:S(2)}) collective-permute-start(bf16[16,4608]{1,0:T(8,128)(2,1)S(1)} %copy-done.2), channel_id=1, source_target_pairs={{0,4},{4,8},{8,12},{12,0},{1,5},{5,9},{9,13},{13,1},{2,6},{6,10},{... | collective-permute-start | bytes 442376 | tf_op jit(solution)/shard_map/while/body/eval_jaxpr/ppermute | solution.py:10
  22.6 7.2 %copy-start.3 = (s32[256]{0:T(256)S(1)}, s32[256]{0:T(256)}, u32[]{:S(2)}) copy-start(s32[256]{0:T(256)} %param.11) | copy-start | bytes 3076
  22.6 7.3 %copy-start.4 = (s32[256]{0:T(256)S(1)}, s32[256]{0:T(256)}, u32[]{:S(2)}) copy-start(s32[256]{0:T(256)} %param.13) | copy-start | bytes 3076
  22.6 7.5 %copy-start.5 = (s32[4,4]{1,0:T(4,128)S(1)}, s32[4,4]{1,0:T(4,128)}, u32[]{:S(2)}) copy-start(s32[4,4]{1,0:T(4,128)} %param.17) | copy-start | bytes 196
  26.0 13.0 %collective-permute-start.2 = (bf16[64,512]{1,0:T(8,128)(2,1)S(1)}, bf16[64,512]{1,0:T(8,128)(2,1)S(1)}, u32[]{:S(2)}, u32[]{:S(2)}) collective-permute-start(bf16[64,512]{1,0:T(8,128)(2,1)S(1)} %copy_bitcast_fusion), channel_id=1, source_target_pairs={{0,12},{4,0},{8,4},{12,8},{1,13},{5,1},{9,5},{13,9},{2,14},{6,2},{... | collective-permute-start | bytes 196616 | tf_op jit(solution)/shard_map/while/body/eval_jaxpr/ppermute | solution.py:10
  29.8 7.9 %collective-permute-start = (bf16[64,512]{1,0:T(8,128)(2,1)S(1)}, bf16[64,512]{1,0:T(8,128)(2,1)S(1)}, u32[]{:S(2)}, u32[]{:S(2)}) collective-permute-start(bf16[64,512]{1,0:T(8,128)(2,1)S(1)} %copy_bitcast_fusion), channel_id=1, source_target_pairs={{0,4},{4,8},{8,12},{12,0},{1,5},{5,9},{9,13},{13,1},{2,6},{6,10},{... | collective-permute-start | bytes 196616 | tf_op jit(solution)/shard_map/while/body/eval_jaxpr/ppermute | solution.py:10
  37.8 7.0 %collective-permute-start.4 = (bf16[64,512]{1,0:T(8,128)(2,1)S(1)}, bf16[64,512]{1,0:T(8,128)(2,1)S(1)}, u32[]{:S(2)}, u32[]{:S(2)}) collective-permute-start(bf16[64,512]{1,0:T(8,128)(2,1)S(1)} %collective-permute-done), channel_id=1, source_target_pairs={{0,4},{4,8},{8,12},{12,0},{1,5},{5,9},{9,13},{13,1},{2,6},{6,10},{... | collective-permute-start | bytes 196616 | tf_op jit(solution)/shard_map/ppermute | solution.py:10
  44.8 204.7 %collective-permute-start.5 = (bf16[16,4608]{1,0:T(8,128)(2,1)S(1)}, bf16[16,4608]{1,0:T(8,128)(2,1)S(1)}, u32[]{:S(2)}, u32[]{:S(2)}) collective-permute-start(bf16[16,4608]{1,0:T(8,128)(2,1)S(1)} %collective-permute-done.1), channel_id=1, source_target_pairs={{0,4},{4,8},{8,12},{12,0},{1,5},{5,9},{9,13},{13,1},{2,6},{6,10},{... | collective-permute-start | bytes 442376 | tf_op jit(solution)/shard_map/ppermute | solution.py:10
  244.5 1.8 copy-start
  250.3 0.7 copy-start.1
Sparse Core Ops, SparseCore 0:
  8.9 33.7 all-gather.3
  44.2 24.5 all-gather.5
  70.4 166.7 all-gather.7
  251.1 18.2 reduce-scatter.1
where the time goes:
time: 278 us; the launch traced here: 277 us
  waiting for transfers between devices  216 us (78%)
  between operations  16 us (6%)
  matrix products  14.3 us (5%)
  starting transfers between devices  10.4 us (4%)
  local copies, waits for them, and re-layouts  9.07 us (3%)
  blocking collectives  7.51 us (3%)
  other arithmetic  4.37 us (2%)
    all_gather x1, waiting for transfers between devices, shards(): lax.all_gather(out_proj, 'tgt', axis=1, tiled=True)  168 us
    reduce_scatter x1, waiting for transfers between devices, shards(): lax.psum_scatter(partial_value, 'src', scatter_dimension=0, tiled=True)  18.4 us
    all_gather x1, waiting for transfers between devices, shards(): lax.all_gather(target_rows, 'src', axis=0, tiled=True)  17.4 us
    ppermute x6, starting transfers between devices, passed_along(): return lax.ppermute(value, axis, pairs)  10.2 us
    ppermute x6, waiting for transfers between devices, passed_along(): return lax.ppermute(value, axis, pairs)  10.2 us
    all_gather x1, blocking collectives, shards(): lax.all_gather(decoder_rows, 'src', axis=0, tiled=True)  7.51 us
    dot_general x1, matrix products, shards(): jnp.einsum('td,hde->the', full_targets, lax.all_gather(out_proj, 'tgt', a...  6.99 us
  transfers between devices with their start and end apart: 10, of which 5 were waited for; matrix products, arithmetic and copies ran while one was open for 8% of the time, Pallas kernels for 0%

commit v1 on v0

--- a/solution.py
+++ b/solution.py
@@ -27,12 +27,27 @@
     head_dim = out_proj.shape[2]
     groups_here = value_proj.shape[0]
     repeat = heads_here // groups_here
-    read_sum = jnp.einsum(
+    count_2, index = (lax.axis_size("tgt"), lax.axis_index("tgt"))
+    left = [(i, (i - 1) % count_2) for i in range(count_2)]
+    span = out_proj.shape[1]
+    held = out_proj
+    running_2 = jnp.einsum(
         "td,hde->the",
-        full_targets,
-        lax.all_gather(out_proj, "tgt", axis=1, tiled=True),
+        lax.dynamic_slice_in_dim(full_targets, index * span, held.shape[1], axis=1),
+        held,
         preferred_element_type=jnp.float32,
     )
+    for turn in range(1, count_2):
+        held = lax.ppermute(held, "tgt", left)
+        running_2 = running_2 + jnp.einsum(
+            "td,hde->the",
+            lax.dynamic_slice_in_dim(
+                full_targets, (index + turn) % count_2 * span, held.shape[1], axis=1
+            ),
+            held,
+            preferred_element_type=jnp.float32,
+        )
+    read_sum = running_2
     head_reads = read_sum.astype(jnp.bfloat16).reshape(tgt_dev, groups_here, repeat, head_dim)
     values = jnp.einsum("sd,gde->sge", full_sources, value_proj, preferred_element_type=jnp.float32)
     values = values.astype(jnp.bfloat16).reshape(src_dev, groups_here * head_dim)

time: 278 us -> 257 us (0.924)
  waiting for transfers between devices: 216 us -> 169 us
  starting transfers between devices: 10.4 us -> 21.6 us
  local copies, waits for them, and re-layouts: 9.07 us -> 15 us
  matrix products: 14.3 us -> 19.8 us
  other arithmetic: 4.37 us -> 7.33 us
    all_gather x1 -> x0, waiting for transfers between devices: 168 us -> none  [shards(): lax.all_gather(out_proj, 'tgt', axis=1, tiled=True)]
    ppermute x0 -> x3, waiting for transfers between devices: none -> 100 us  [shards(): held = lax.ppermute(held, 'tgt', left)]
    ppermute x6, waiting for transfers between devices: 10.2 us -> 49 us  [passed_along(): return lax.ppermute(value, axis, pairs)]
    all_gather x1, waiting for transfers between devices: 17.4 us -> 0.01 us  [shards(): lax.all_gather(target_rows, 'src', axis=0, tiled=True)]
    ppermute x0 -> x3, starting transfers between devices: none -> 13.6 us  [shards(): held = lax.ppermute(held, 'tgt', left)]
    dot_general x4, matrix products: 2.81 us -> 6.47 us  [edge_tile(): jnp.einsum('sd,td->st', decoder_part, full_targets, preferred_element_typ...]
    gather x4, local copies, waits for them, and re-layouts: 2.38 us -> 5.46 us  [edge_tile(): weights = jnp.take(keyed_attn, key_positions, axis=1).astype(jnp.float32)]
    dot_general x1 -> x4, matrix products: 6.99 us -> 8.77 us  [the longest x3 5.94 us: shards(): jnp.einsum('td,hde->the', lax.dynamic_slice_in_dim(full_targets, (index +...]
  transfers between devices with their start and end apart: 10 -> 12, of which waited for: 5 -> 4; matrix products, arithmetic and copies ran while one was open for 8% -> 15% of each run, Pallas kernels for 0% -> 0%
where the time goes in v1:
time: 257 us
  waiting for transfers between devices  169 us (66%)
  starting transfers between devices  21.6 us (8%)
  matrix products  19.8 us (8%)
  between operations  16.1 us (6%)
  local copies, waits for them, and re-layouts  15 us (6%)
  blocking collectives  7.75 us (3%)
  other arithmetic  7.33 us (3%)
    ppermute x3, waiting for transfers between devices, shards(): held = lax.ppermute(held, 'tgt', left)  100 us
    ppermute x6, waiting for transfers between devices, passed_along(): return lax.ppermute(value, axis, pairs)  49 us
    reduce_scatter x1, waiting for transfers between devices, shards(): lax.psum_scatter(partial_value, 'src', scatter_dimension=0, tiled=True)  19.9 us
    ppermute x3, starting transfers between devices, shards(): held = lax.ppermute(held, 'tgt', left)  13.6 us
    ppermute x6, starting transfers between devices, passed_along(): return lax.ppermute(value, axis, pairs)  7.83 us
    all_gather x1, blocking collectives, shards(): lax.all_gather(decoder_rows, 'src', axis=0, tiled=True)  7.75 us
    dot_general x4, matrix products, edge_tile(): jnp.einsum('sd,td->st', decoder_part, full_targets, preferred_element_typ...  6.47 us
    dot_general x3, matrix products, shards(): jnp.einsum('td,hde->the', lax.dynamic_slice_in_dim(full_targets, (index +...  5.94 us
  transfers between devices with their start and end apart: 12, of which 4 were waited for; matrix products, arithmetic and copies ran while one was open for 15% of the time, Pallas kernels for 0%

profile of v1, /device:TPU:0, one launch (start us, length us, event | category | flops | bytes accessed | tf_op | source)
XLA Modules:
  0.0 256.8 jit_solution(4101901621774456490)
XLA Ops:
  6.5 5.1 %collective-permute-start = (bf16[8,1152,128]{2,1,0:T(8,128)(2,1)}, bf16[8,1152,128]{2,1,0:T(8,128)(2,1)S(1)}, u32[]{:S(2)}, u32[]{:S(2)}) collective-permute-start(bf16[8,1152,128]{2,1,0:T(8,128)(2,1)} %param.14), channel_id=1, source_target_pairs={{0,12},{4,0},{8,4},{12,8},{1,13},{5,1},{9,5},{13,9},{2,14},{6,2},{... | collective-permute-start | bytes 7077896 | tf_op jit(solution)/shard_map/ppermute | solution.py:41
  11.6 1.8 copy.26
  13.5 65.8 %collective-permute-done = bf16[8,1152,128]{2,1,0:T(8,128)(2,1)S(1)} collective-permute-done((bf16[8,1152,128]{2,1,0:T(8,128)(2,1)}, bf16[8,1152,128]{2,1,0:T(8,128)(2,1)S(1)}, u32[]{:S(2)}, u32[]{:S(2)}) %collective-permute-start) | collective-permute-done | bytes 2359328 | tf_op jit(solution)/shard_map/ppermute | solution.py:41
  79.3 4.2 %collective-permute-start.1 = (bf16[8,1152,128]{2,1,0:T(8,128)(2,1)S(1)}, bf16[8,1152,128]{2,1,0:T(8,128)(2,1)}, u32[]{:S(2)}, u32[]{:S(2)}) collective-permute-start(bf16[8,1152,128]{2,1,0:T(8,128)(2,1)S(1)} %collective-permute-done), channel_id=1, source_target_pairs={{0,12},{4,0},{8,4},{12,8},{1,13},{5,1},{9,5},{13,9},{2,14},{6,2},{... | collective-permute-start | bytes 7077896 | tf_op jit(solution)/shard_map/ppermute | solution.py:41
  83.6 7.7 %all_gather.11 = bf16[64,4608]{1,0:T(8,128)(2,1)S(1)} all-gather(bf16[16,4608]{1,0:T(8,128)(2,1)} %param.12), channel_id=1, replica_groups=mesh['grp'=2,'tgt'=4,'src'=4] {'src'}, dimensions={0}, use_global_device_ids=true | all-gather | bytes 737280 | tf_op jit(solution)/shard_map/all_gather | solution.py:21
  91.4 3.3 %convolution_convert_fusion = bf16[64,4,128]{2,0,1:T(8,128)(2,1)S(1)} fusion(bf16[4,4608,128]{2,1,0:T(8,128)(2,1)} %param.15, bf16[64,4608]{1,0:T(8,128)(2,1)S(1)} %all_gather.11), kind=kOutput, calls=%fused_computation.9 | convolution fusion | flops 302022656 | bytes 5373952 | tf_op jit(solution)/shard_map/sd,gde->sge/dot_general | solution.py:52
  94.8 3.9 %collective-permute-start.5 = (bf16[64,512]{1,0:T(8,128)(2,1)S(1)}, bf16[64,512]{1,0:T(8,128)(2,1)S(1)}, u32[]{:S(2)}, u32[]{:S(2)}) collective-permute-start(bf16[64,512]{1,0:T(8,128)(2,1)S(1)} %copy_bitcast_fusion), channel_id=1, source_target_pairs={{0,12},{4,0},{8,4},{12,8},{1,13},{5,1},{9,5},{13,9},{2,14},{6,2},{... | collective-permute-start | bytes 196616 | tf_op jit(solution)/shard_map/while/body/eval_jaxpr/ppermute | solution.py:10
  98.6 2.0 collective-permute-start.6
  100.6 34.5 %collective-permute-done.1 = bf16[8,1152,128]{2,1,0:T(8,128)(2,1)} collective-permute-done((bf16[8,1152,128]{2,1,0:T(8,128)(2,1)S(1)}, bf16[8,1152,128]{2,1,0:T(8,128)(2,1)}, u32[]{:S(2)}, u32[]{:S(2)}) %collective-permute-start.1) | collective-permute-done | bytes 2359328 | tf_op jit(solution)/shard_map/ppermute | solution.py:41
  135.1 4.4 %collective-permute-start.2 = (bf16[8,1152,128]{2,1,0:T(8,128)(2,1)}, bf16[8,1152,128]{2,1,0:T(8,128)(2,1)}, u32[]{:S(2)}, u32[]{:S(2)}) collective-permute-start(bf16[8,1152,128]{2,1,0:T(8,128)(2,1)} %collective-permute-done.1), channel_id=1, source_target_pairs={{0,12},{4,0},{8,4},{12,8},{1,13},{5,1},{9,5},{13,9},{2,14},{6,2},{... | collective-permute-start | bytes 7077896 | tf_op jit(solution)/shard_map/ppermute | solution.py:41
  146.0 49.0 %collective-permute-done.7 = bf16[64,512]{1,0:T(8,128)(2,1)S(1)} collective-permute-done((bf16[64,512]{1,0:T(8,128)(2,1)S(1)}, bf16[64,512]{1,0:T(8,128)(2,1)S(1)}, u32[]{:S(2)}, u32[]{:S(2)}) %collective-permute-start.7) | collective-permute-done | bytes 65568 | tf_op jit(solution)/shard_map/ppermute | solution.py:10
  195.6 1.8 collective-permute-start.8
  197.5 2.0 gather_fusion
  199.5 2.2 select_bitcast_fusion
  201.7 2.2 copy.27
  209.4 2.8 %fusion.13 = f32[256,8,128]{2,0,1:T(8,128)S(1)} fusion(bf16[8,1152,128]{2,1,0:T(8,128)(2,1)} %param.14, bf16[256,4608]{1,0:T(8,128)(2,1)} %all-gather.5.cloned.1.call-done, s32[]{:T(128)S(6)} %select_n.126), kind=kOutput, calls=%fused_computation.27 | convolution fusion | flops 603979776 | bytes 3997700 | tf_op jit(solution)/shard_map/td,hde->the/dot_general | solution.py:34
  213.1 2.5 convolution_add_fusion.1
  215.6 2.6 fusion
  220.4 1.6 fusion.8
  222.2 1.6 fusion.6
  224.3 1.6 fusion.4
  226.4 1.6 fusion.2
  228.8 19.9 %reduce-scatter.2.cloned.1.call-done = f32[64,256]{1,0:T(8,128)} async-done(((f32[256,256]{1,0:T(8,128)}), f32[64,256]{1,0:T(8,128)}) %reduce-scatter.2.cloned.1.call-update) | async-done | bytes 65552 | tf_op jit(solution)/shard_map/reduce_scatter | solution.py:103
  248.8 1.5 convert_element_type.69
  (86 shorter events, 15.0 us)
Async XLA Ops:
  6.5 190.9 %all-gather.3.cloned.1.call-start = ((), (), s32[]{:S(2)}) async-start(), calls=%async_computation.1 | async-start | bytes 1310720 | tf_op jit(solution)/shard_map/all_gather | solution.py:54
  6.5 72.8 %collective-permute-start = (bf16[8,1152,128]{2,1,0:T(8,128)(2,1)}, bf16[8,1152,128]{2,1,0:T(8,128)(2,1)S(1)}, u32[]{:S(2)}, u32[]{:S(2)}) collective-permute-start(bf16[8,1152,128]{2,1,0:T(8,128)(2,1)} %param.14), channel_id=1, source_target_pairs={{0,12},{4,0},{8,4},{12,8},{1,13},{5,1},{9,5},{13,9},{2,14},{6,2},{... | collective-permute-start | bytes 7077896 | tf_op jit(solution)/shard_map/ppermute | solution.py:41
  13.5 195.9 %all-gather.5.cloned.1.call-start = ((), (), s32[]{:S(2)}) async-start(), calls=%async_computation.2 | async-start | bytes 2949120 | tf_op jit(solution)/shard_map/all_gather | solution.py:20
  79.3 55.8 %collective-permute-start.1 = (bf16[8,1152,128]{2,1,0:T(8,128)(2,1)S(1)}, bf16[8,1152,128]{2,1,0:T(8,128)(2,1)}, u32[]{:S(2)}, u32[]{:S(2)}) collective-permute-start(bf16[8,1152,128]{2,1,0:T(8,128)(2,1)S(1)} %collective-permute-done), channel_id=1, source_target_pairs={{0,12},{4,0},{8,4},{12,8},{1,13},{5,1},{9,5},{13,9},{2,14},{6,2},{... | collective-permute-start | bytes 7077896 | tf_op jit(solution)/shard_map/ppermute | solution.py:41
  83.5 165.3 %reduce-scatter.2.cloned.1.call-start = ((), (), s32[]{:S(2)}) async-start(), calls=%async_computation.3 | async-start | bytes 327680 | tf_op jit(solution)/shard_map/reduce_scatter | solution.py:103
  83.5 112.1 %collective-permute-start.4 = (bf16[16,4608]{1,0:T(8,128)(2,1)}, bf16[16,4608]{1,0:T(8,128)(2,1)}, u32[]{:S(2)}, u32[]{:S(2)}) collective-permute-start(bf16[16,4608]{1,0:T(8,128)(2,1)} %param.12), channel_id=1, source_target_pairs={{0,4},{4,8},{8,12},{12,0},{1,5},{5,9},{9,13},{13,1},{2,6},{6,10},{... | collective-permute-start | bytes 442376 | tf_op jit(solution)/shard_map/while/body/eval_jaxpr/ppermute | solution.py:10
  91.4 48.1 %copy-start.8 = (s32[256]{0:T(256)S(1)}, s32[256]{0:T(256)}, u32[]{:S(2)}) copy-start(s32[256]{0:T(256)} %param.11) | copy-start | bytes 3076
  91.4 48.2 %copy-start.9 = (s32[256]{0:T(256)S(1)}, s32[256]{0:T(256)}, u32[]{:S(2)}) copy-start(s32[256]{0:T(256)} %param.13) | copy-start | bytes 3076
  91.4 50.0 %copy-start.14 = (s32[4,4]{1,0:T(4,128)S(1)}, s32[4,4]{1,0:T(4,128)}, u32[]{:S(2)}) copy-start(s32[4,4]{1,0:T(4,128)} %param.17) | copy-start | bytes 196
  94.7 49.9 %collective-permute-start.3 = (bf16[64,512]{1,0:T(8,128)(2,1)S(1)}, bf16[64,512]{1,0:T(8,128)(2,1)S(1)}, u32[]{:S(2)}, u32[]{:S(2)}) collective-permute-start(bf16[64,512]{1,0:T(8,128)(2,1)S(1)} %copy_bitcast_fusion), channel_id=1, source_target_pairs={{0,4},{4,8},{8,12},{12,0},{1,5},{5,9},{9,13},{13,1},{2,6},{6,10},{... | collective-permute-start | bytes 196616 | tf_op jit(solution)/shard_map/while/body/eval_jaxpr/ppermute | solution.py:10
  94.8 50.6 %collective-permute-start.5 = (bf16[64,512]{1,0:T(8,128)(2,1)S(1)}, bf16[64,512]{1,0:T(8,128)(2,1)S(1)}, u32[]{:S(2)}, u32[]{:S(2)}) collective-permute-start(bf16[64,512]{1,0:T(8,128)(2,1)S(1)} %copy_bitcast_fusion), channel_id=1, source_target_pairs={{0,12},{4,0},{8,4},{12,8},{1,13},{5,1},{9,5},{13,9},{2,14},{6,2},{... | collective-permute-start | bytes 196616 | tf_op jit(solution)/shard_map/while/body/eval_jaxpr/ppermute | solution.py:10
  98.6 125.7 %collective-permute-start.6 = (bf16[16,4608]{1,0:T(8,128)(2,1)}, bf16[16,4608]{1,0:T(8,128)(2,1)}, u32[]{:S(2)}, u32[]{:S(2)}) collective-permute-start(bf16[16,4608]{1,0:T(8,128)(2,1)} %param.12), channel_id=1, source_target_pairs={{0,12},{4,0},{8,4},{12,8},{1,13},{5,1},{9,5},{13,9},{2,14},{6,2},{... | collective-permute-start | bytes 442376 | tf_op jit(solution)/shard_map/while/body/eval_jaxpr/ppermute | solution.py:10
  135.1 80.5 %collective-permute-start.2 = (bf16[8,1152,128]{2,1,0:T(8,128)(2,1)}, bf16[8,1152,128]{2,1,0:T(8,128)(2,1)}, u32[]{:S(2)}, u32[]{:S(2)}) collective-permute-start(bf16[8,1152,128]{2,1,0:T(8,128)(2,1)} %collective-permute-done.1), channel_id=1, source_target_pairs={{0,12},{4,0},{8,4},{12,8},{1,13},{5,1},{9,5},{13,9},{2,14},{6,2},{... | collective-permute-start | bytes 7077896 | tf_op jit(solution)/shard_map/ppermute | solution.py:41
  144.6 50.4 %collective-permute-start.7 = (bf16[64,512]{1,0:T(8,128)(2,1)S(1)}, bf16[64,512]{1,0:T(8,128)(2,1)S(1)}, u32[]{:S(2)}, u32[]{:S(2)}) collective-permute-start(bf16[64,512]{1,0:T(8,128)(2,1)S(1)} %collective-permute-done.3), channel_id=1, source_target_pairs={{0,4},{4,8},{8,12},{12,0},{1,5},{5,9},{9,13},{13,1},{2,6},{6,10},{... | collective-permute-start | bytes 196616 | tf_op jit(solution)/shard_map/ppermute | solution.py:10
  195.6 30.8 %collective-permute-start.8 = (bf16[16,4608]{1,0:T(8,128)(2,1)}, bf16[16,4608]{1,0:T(8,128)(2,1)}, u32[]{:S(2)}, u32[]{:S(2)}) collective-permute-start(bf16[16,4608]{1,0:T(8,128)(2,1)} %collective-permute-done.4), channel_id=1, source_target_pairs={{0,4},{4,8},{8,12},{12,0},{1,5},{5,9},{9,13},{13,1},{2,6},{6,10},{... | collective-permute-start | bytes 442376 | tf_op jit(solution)/shard_map/ppermute | solution.py:10
  209.3 2.8 %copy-start = (bf16[256,4608]{1,0:T(8,128)(2,1)S(1)}, bf16[256,4608]{1,0:T(8,128)(2,1)}, u32[]{:S(2)}) copy-start(bf16[256,4608]{1,0:T(8,128)(2,1)} %all-gather.5.cloned.1.call-done) | copy-start | bytes 7077892
  215.6 2.9 %copy-start.7 = (bf16[64,4,128]{2,1,0:T(4,128)(2,1)S(1)}, bf16[64,4,128]{2,1,0:T(4,128)(2,1)}, u32[]{:S(2)}) copy-start(bf16[64,4,128]{2,1,0:T(4,128)(2,1)} %reshape.57) | copy-start | bytes 196612
  215.6 3.3 %copy-start.6 = (bf16[64,4,128]{2,1,0:T(4,128)(2,1)S(1)}, bf16[64,4,128]{2,1,0:T(4,128)(2,1)}, u32[]{:S(2)}) copy-start(bf16[64,4,128]{2,1,0:T(4,128)(2,1)} %reshape.55) | copy-start | bytes 196612
  219.5 2.7 %copy-start.17 = (s32[16]{0:T(128)S(1)}, s32[16]{0:T(128)}, u32[]{:S(2)}) copy-start(s32[16]{0:T(128)} %get-tuple-element.65) | copy-start | bytes 196
  220.4 3.4 %copy-start.2 = (bf16[64,8,256]{2,1,0:T(8,128)(2,1)S(1)}, bf16[64,8,256]{2,1,0:T(8,128)(2,1)}, u32[]{:S(2)}) copy-start(bf16[64,8,256]{2,1,0:T(8,128)(2,1)} %gather_fusion.3) | copy-start | bytes 786436
  220.4 3.4 %copy-start.11 = (pred[64]{0:T(512)(128)(4,1)S(1)}, pred[64]{0:T(512)(128)(4,1)}, u32[]{:S(2)}) copy-start(pred[64]{0:T(512)(128)(4,1)} %get-tuple-element.67) | copy-start | bytes 196
  222.1 2.2 copy-start.16
  223.8 2.2 copy-start.10
  223.8 2.6 %copy-start.15 = (s32[16]{0:T(128)S(1)}, s32[16]{0:T(128)}, u32[]{:S(2)}) copy-start(s32[16]{0:T(128)} %get-tuple-element.62) | copy-start | bytes 196
  (7 other events, 10.2 us)
Sparse Core Ops, SparseCore 0:
  13.6 40.0 all-gather.2
  83.6 23.4 all-gather.4
  228.9 19.7 reduce-scatter.1
